TPU v7x, 32 devices: a whole 2x2x4 slice. The times are simulated.
32 devices in a mesh: rows: 8 (over z, y), grp: 4 (over x, core).
Axes of the slice: x: 2, y: 2, z: 4, core: 2. Of those that a mesh axis runs over, the one named last changes fastest.
Arguments:
- basis: float32 [32, 65536], P(None, ('rows', 'grp')), may hold values from -0.03125 to 0.03125, as said below
- core: float32 [32, 32], replicated, may hold values from -0.3 to 4
- snapshots: bfloat16 [4, 32, 65536], P(None, 'grp', 'rows'), may hold values from -16 to 16
Outputs:
- new_basis: float32 [32, 65536], P(None, ('rows', 'grp'))
- new_core: float32 [32, 32], replicated
- first_coeffs: float32 [4, 32, 32], replicated
Inputs may be any that keep to these rules, and one draw needn't show every extreme that they name: `basis`: rows orthonormal up to float32 rounding.
All inputs are finite; a program needn't handle non-finite values.
Results may differ from a plain program's by a relative error of at most 0.0003.
Values may be sent and summed in bfloat16 or wider, within the bound.
A program may use at most 64 MiB of HBM per device.

v0:
```python
import jax
import jax.numpy as jnp
from jax import lax
from jax.sharding import PartitionSpec as P

BATCHES = 4
epsilon = 1e-06


def contract_rows(left, right):
    return lax.dot_general(
        left,
        right,
        (((1,), (1,)), ((), ())),
        precision=lax.Precision.HIGHEST,
        preferred_element_type=jnp.float32,
    )


def matmul(left, right):
    return jnp.dot(left, right, precision=lax.Precision.HIGHEST, preferred_element_type=jnp.float32)


def lower_solve(factor, right):
    return lax.linalg.triangular_solve(factor, right, left_side=True, lower=True)


def small_update(core_now, total, lower):
    rank = core_now.shape[0]
    cols = lower.shape[0]
    top = jnp.concatenate([core_now, total], axis=1)
    bottom = jnp.concatenate([jnp.zeros((cols, rank), jnp.float32), lower.T], axis=1)
    stacked = jnp.concatenate([top, bottom], axis=0)
    moment = matmul(stacked, stacked.T)
    leading = moment[:, :rank]
    factor = jnp.linalg.cholesky(matmul(leading.T, leading))
    rotation = lower_solve(factor, leading.T).T
    fresh_core = jnp.linalg.cholesky(matmul(rotation.T, matmul(moment, rotation)))
    return (rotation, fresh_core)


def body(basis, core, snapshots):
    rank = basis.shape[0]
    basis_now = basis
    core_now = core
    firsts = []
    gram_basis = lax.psum(contract_rows(basis_now, basis_now), ("rows", "grp"))
    for batch in range(BATCHES):
        columns = lax.all_to_all(snapshots[batch], "grp", split_axis=1, concat_axis=0, tiled=True)
        raw = columns.astype(jnp.float32)
        raw_cross, raw_gram = lax.psum(
            (contract_rows(basis_now, raw), contract_rows(raw, raw)), ("rows", "grp")
        )
        inverse = lax.rsqrt(jnp.diagonal(raw_gram) + epsilon)
        scaled = raw * inverse[:, None]
        cross = raw_cross * inverse[None, :]
        gram_raw = raw_gram * inverse[:, None] * inverse[None, :]
        second = cross - matmul(gram_basis, cross)
        total = cross + second
        basis_cross = cross - matmul(gram_basis, total)
        gram = (
            gram_raw
            - matmul(total.T, cross)
            - matmul(cross.T, total)
            + matmul(total.T, matmul(gram_basis, total))
        )
        twice = scaled - matmul(total.T, basis_now)
        lower = jnp.linalg.cholesky(gram)
        fresh = lower_solve(lower, twice)
        rotation, core_now = small_update(core_now, total, lower)
        cross_fresh = lower_solve(lower, basis_cross.T).T
        halfway = lower_solve(lower, gram)
        gram_fresh = lower_solve(lower, halfway.T).T
        upper_block = jnp.concatenate([gram_basis, cross_fresh], axis=1)
        lower_block = jnp.concatenate([cross_fresh.T, gram_fresh], axis=1)
        combined = jnp.concatenate([upper_block, lower_block], axis=0)
        gram_basis = matmul(rotation.T, matmul(combined, rotation))
        firsts.append(cross)
        basis_now = matmul(rotation[:rank].T, basis_now) + matmul(rotation[rank:].T, fresh)
    return (basis_now, core_now, jnp.stack(firsts, axis=0))


def solution(mesh):
    return jax.shard_map(
        body,
        mesh=mesh,
        in_specs=(P(None, ("rows", "grp")), P(), P(None, "grp", "rows")),
        out_specs=(P(None, ("rows", "grp")), P(), P()),
        check_vma=False,
    )
```

profile of v0, /device:TPU:0, one launch (start us, length us, event | category | flops | bytes accessed | tf_op | source)
XLA Modules:
  0.0 283.6 jit_solution(1562950860485663812)
XLA Ops:
  0.6 1.9 fusion.229
  2.6 4.4 %all-to-all-start = ((bf16[8,4,2048]{2,0,1:T(8,128)(2,1)}), bf16[8,4,2048]{2,0,1:T(8,128)(2,1)S(1)}, u32[]{:S(2)}, u32[]{:S(2)}) async-start(bf16[8,4,2048]{2,0,1:T(8,128)(2,1)} %bitcast), calls=%async_computation | async-start | bytes 262144 | tf_op jit(solution)/shard_map/all_to_all | solution.py:49
  7.4 4.1 %all-to-all-done = bf16[8,4,2048]{2,0,1:T(8,128)(2,1)S(1)} async-done(((bf16[8,4,2048]{2,0,1:T(8,128)(2,1)}), bf16[8,4,2048]{2,0,1:T(8,128)(2,1)S(1)}, u32[]{:S(2)}, u32[]{:S(2)}) %all-to-all-start) | async-done | bytes 131104 | tf_op jit(solution)/shard_map/all_to_all | solution.py:49
  11.6 3.3 %all-to-all-start.1 = ((bf16[8,4,2048]{2,0,1:T(8,128)(2,1)}), bf16[8,4,2048]{2,0,1:T(8,128)(2,1)S(1)}, u32[]{:S(2)}, u32[]{:S(2)}) async-start(bf16[8,4,2048]{2,0,1:T(8,128)(2,1)} %bitcast.15), calls=%async_computation.1 | async-start | bytes 262144 | tf_op jit(solution)/shard_map/all_to_all | solution.py:49
  15.3 42.1 %all-reduce.7 = (f32[32,32]{1,0:T(8,128)S(1)}, f32[32,32]{0,1:T(8,128)S(1)}, f32[32,32]{0,1:T(8,128)S(1)}) all-reduce(f32[32,32]{1,0:T(8,128)S(1)} %fusion.230, f32[32,32]{0,1:T(8,128)S(1)} %fusion.18, f32[32,32]{0,1:T(8,128)S(1)} %fusion.16), channel_id=1, replica_groups=mesh['rows'=8,'grp'=4] {'rows','grp'}, use_global_device_ids=true, to_apply=%region_2.0 | all-reduce | flops 3072 | bytes 24576 | tf_op jit(solution)/shard_map/psum | solution.py:47
  59.3 2.9 %cholesky.194 = f32[32,32]{1,0:T(8,128)S(1)} custom-call(f32[32,32]{1,0:T(8,128)S(1)} %fusion.134), custom_call_target="Cholesky" | custom-call | tf_op jit(solution)/shard_map/jit(cholesky)/cholesky | solution.py:68
  63.6 2.4 custom-call.34
  67.2 2.9 %cholesky.205 = f32[32,32]{1,0:T(8,128)S(1)} custom-call(f32[32,32]{1,0:T(8,128)S(1)} %fusion.133), custom_call_target="Cholesky" | custom-call | tf_op jit(solution)/shard_map/jit(cholesky)/cholesky | solution.py:36
  71.4 2.4 custom-call.33
  76.5 3.5 %all-to-all-start.2 = ((bf16[8,4,2048]{2,0,1:T(8,128)(2,1)}), bf16[8,4,2048]{2,0,1:T(8,128)(2,1)S(1)}, u32[]{:S(2)}, u32[]{:S(2)}) async-start(bf16[8,4,2048]{2,0,1:T(8,128)(2,1)} %bitcast.39), calls=%async_computation.2 | async-start | bytes 262144 | tf_op jit(solution)/shard_map/all_to_all | solution.py:49
  80.4 41.5 %all-reduce.6 = (f32[32,32]{0,1:T(8,128)S(1)}, f32[32,32]{0,1:T(8,128)S(1)}) all-reduce(f32[32,32]{0,1:T(8,128)S(1)} %fusion.14, f32[32,32]{0,1:T(8,128)S(1)} %fusion.12), channel_id=1, replica_groups=mesh['rows'=8,'grp'=4] {'rows','grp'}, use_global_device_ids=true, to_apply=%region_5.9 | all-reduce | flops 2048 | bytes 16384 | tf_op jit(solution)/shard_map/psum | solution.py:51
  123.5 2.9 %cholesky.216 = f32[32,32]{1,0:T(8,128)S(1)} custom-call(f32[32,32]{1,0:T(8,128)S(1)} %fusion.129), custom_call_target="Cholesky" | custom-call | tf_op jit(solution)/shard_map/jit(cholesky)/cholesky | solution.py:38
  128.5 2.9 %cholesky.227 = f32[32,32]{1,0:T(8,128)S(1)} custom-call(f32[32,32]{1,0:T(8,128)S(1)} %fusion.121), custom_call_target="Cholesky" | custom-call | tf_op jit(solution)/shard_map/jit(cholesky)/cholesky | solution.py:68
  132.8 2.4 custom-call.39
  136.4 2.9 %cholesky.238 = f32[32,32]{1,0:T(8,128)S(1)} custom-call(f32[32,32]{1,0:T(8,128)S(1)} %fusion.120), custom_call_target="Cholesky" | custom-call | tf_op jit(solution)/shard_map/jit(cholesky)/cholesky | solution.py:36
  140.7 2.4 custom-call.38
  145.7 3.5 %all-to-all-start.3 = ((bf16[8,4,2048]{2,0,1:T(8,128)(2,1)}), bf16[8,4,2048]{2,0,1:T(8,128)(2,1)S(1)}, u32[]{:S(2)}, u32[]{:S(2)}) async-start(bf16[8,4,2048]{2,0,1:T(8,128)(2,1)} %bitcast.63), calls=%async_computation.3 | async-start | bytes 262144 | tf_op jit(solution)/shard_map/all_to_all | solution.py:49
  149.7 40.7 %all-reduce.5 = (f32[32,32]{0,1:T(8,128)S(1)}, f32[32,32]{0,1:T(8,128)S(1)}) all-reduce(f32[32,32]{0,1:T(8,128)S(1)} %fusion.10, f32[32,32]{0,1:T(8,128)S(1)} %fusion.8), channel_id=1, replica_groups=mesh['rows'=8,'grp'=4] {'rows','grp'}, use_global_device_ids=true, to_apply=%region_7.12 | all-reduce | flops 2048 | bytes 16384 | tf_op jit(solution)/shard_map/psum | solution.py:51
  192.0 2.9 %cholesky.249 = f32[32,32]{1,0:T(8,128)S(1)} custom-call(f32[32,32]{1,0:T(8,128)S(1)} %fusion.116), custom_call_target="Cholesky" | custom-call | tf_op jit(solution)/shard_map/jit(cholesky)/cholesky | solution.py:38
  197.0 2.9 %cholesky.260 = f32[32,32]{1,0:T(8,128)S(1)} custom-call(f32[32,32]{1,0:T(8,128)S(1)} %fusion.108), custom_call_target="Cholesky" | custom-call | tf_op jit(solution)/shard_map/jit(cholesky)/cholesky | solution.py:68
  201.2 2.4 custom-call.44
  204.8 2.9 %cholesky.271 = f32[32,32]{1,0:T(8,128)S(1)} custom-call(f32[32,32]{1,0:T(8,128)S(1)} %fusion.107), custom_call_target="Cholesky" | custom-call | tf_op jit(solution)/shard_map/jit(cholesky)/cholesky | solution.py:36
  209.1 2.4 custom-call.43
  214.6 39.8 %all-reduce.4 = (f32[32,32]{0,1:T(8,128)S(1)}, f32[32,32]{0,1:T(8,128)S(1)}) all-reduce(f32[32,32]{0,1:T(8,128)S(1)} %fusion.6, f32[32,32]{0,1:T(8,128)S(1)} %fusion.4), channel_id=1, replica_groups=mesh['rows'=8,'grp'=4] {'rows','grp'}, use_global_device_ids=true, to_apply=%region_9.14 | all-reduce | flops 2048 | bytes 16384 | tf_op jit(solution)/shard_map/psum | solution.py:51
  256.1 2.9 %cholesky.282 = f32[32,32]{1,0:T(8,128)S(1)} custom-call(f32[32,32]{1,0:T(8,128)S(1)} %fusion.103), custom_call_target="Cholesky" | custom-call | tf_op jit(solution)/shard_map/jit(cholesky)/cholesky | solution.py:38
  261.8 2.9 %cholesky.293 = f32[32,32]{1,0:T(8,128)S(1)} custom-call(f32[32,32]{1,0:T(8,128)S(1)} %fusion.95), custom_call_target="Cholesky" | custom-call | tf_op jit(solution)/shard_map/jit(cholesky)/cholesky | solution.py:68
  266.0 2.4 custom-call.49
  269.0 2.9 %cholesky.304 = f32[32,32]{1,0:T(8,128)S(1)} custom-call(f32[32,32]{1,0:T(8,128)S(1)} %fusion.94), custom_call_target="Cholesky" | custom-call | tf_op jit(solution)/shard_map/jit(cholesky)/cholesky | solution.py:36
  273.3 2.4 custom-call.48
  276.5 2.9 %cholesky.315 = f32[32,32]{1,0:T(8,128)S(1)} custom-call(f32[32,32]{1,0:T(8,128)S(1)} %fusion.88), custom_call_target="Cholesky" | custom-call | tf_op jit(solution)/shard_map/jit(cholesky)/cholesky | solution.py:38
  280.1 1.3 select_select_fusion.4
  282.5 1.1 convolution_add_fusion
  (170 shorter events, 40.3 us)
Async XLA Ops:
  0.6 6.4 %copy-start = (f32[32,2048]{1,0:T(8,128)S(1)}, f32[32,2048]{1,0:T(8,128)}, u32[]{:S(2)}) copy-start(f32[32,2048]{1,0:T(8,128)} %param.10) | copy-start | bytes 786436
  2.6 4.4 %copy-start.1 = (f32[32,32]{1,0:T(8,128)S(1)}, f32[32,32]{1,0:T(8,128)}, u32[]{:S(2)}) copy-start(f32[32,32]{1,0:T(8,128)} %param.11) | copy-start | bytes 12292
  2.6 9.0 %all-to-all-start = ((bf16[8,4,2048]{2,0,1:T(8,128)(2,1)}), bf16[8,4,2048]{2,0,1:T(8,128)(2,1)S(1)}, u32[]{:S(2)}, u32[]{:S(2)}) async-start(bf16[8,4,2048]{2,0,1:T(8,128)(2,1)} %bitcast), calls=%async_computation | async-start | bytes 262144 | tf_op jit(solution)/shard_map/all_to_all | solution.py:49
  11.6 64.9 %all-to-all-start.1 = ((bf16[8,4,2048]{2,0,1:T(8,128)(2,1)}), bf16[8,4,2048]{2,0,1:T(8,128)(2,1)S(1)}, u32[]{:S(2)}, u32[]{:S(2)}) async-start(bf16[8,4,2048]{2,0,1:T(8,128)(2,1)} %bitcast.15), calls=%async_computation.1 | async-start | bytes 262144 | tf_op jit(solution)/shard_map/all_to_all | solution.py:49
  76.5 69.2 %all-to-all-start.2 = ((bf16[8,4,2048]{2,0,1:T(8,128)(2,1)}), bf16[8,4,2048]{2,0,1:T(8,128)(2,1)S(1)}, u32[]{:S(2)}, u32[]{:S(2)}) async-start(bf16[8,4,2048]{2,0,1:T(8,128)(2,1)} %bitcast.39), calls=%async_computation.2 | async-start | bytes 262144 | tf_op jit(solution)/shard_map/all_to_all | solution.py:49
  145.7 68.5 %all-to-all-start.3 = ((bf16[8,4,2048]{2,0,1:T(8,128)(2,1)}), bf16[8,4,2048]{2,0,1:T(8,128)(2,1)S(1)}, u32[]{:S(2)}, u32[]{:S(2)}) async-start(bf16[8,4,2048]{2,0,1:T(8,128)(2,1)} %bitcast.63), calls=%async_computation.3 | async-start | bytes 262144 | tf_op jit(solution)/shard_map/all_to_all | solution.py:49
where the time goes:
time: 285 us; the launch traced here: 284 us
  blocking collectives  164 us (58%)
  other arithmetic  71.8 us (25%)
  matrix products  20.3 us (7%)
  starting transfers between devices  14.7 us (5%)
  local copies, waits for them, and re-layouts  7.12 us (2%)
  waiting for transfers between devices  4.15 us (1%)
    psum x3, blocking collectives, body(): lax.psum((contract_rows(basis_now, raw), contract_rows(raw, raw)), ('rows...  122 us
    psum x1, blocking collectives, body(): gram_basis = lax.psum(contract_rows(basis_now, basis_now), ('rows', 'grp'))  42.1 us
    another operation x16, other arithmetic, lower_solve(): lax.linalg.triangular_solve(factor, right, left_side=True, lower=True)  24.7 us
    all_to_all x4, starting transfers between devices, body(): lax.all_to_all(snapshots[batch], 'grp', split_axis=1, concat_axis=0, tile...  14.7 us
    another operation x12, other arithmetic, small_update(): jnp.linalg.cholesky(matmul(rotation.T, matmul(moment, rotation)))  14.7 us
    another operation x12, other arithmetic, small_update(): factor = jnp.linalg.cholesky(matmul(leading.T, leading))  14.4 us
    another operation x12, other arithmetic, body(): lower = jnp.linalg.cholesky(gram)  14.4 us
    dot_general x54, matrix products, matmul(): jnp.dot(left, right, precision=lax.Precision.HIGHEST, preferred_element_t...  13.7 us
  transfers between devices with their start and end apart: 4, of which 1 were waited for; matrix products, arithmetic and copies ran while one was open for 24% of the time, Pallas kernels for 0%

commit v1 on v0

--- a/solution.py
+++ b/solution.py
@@ -44,7 +44,9 @@
     basis_now = basis
     core_now = core
     firsts = []
-    gram_basis = lax.psum(contract_rows(basis_now, basis_now), ("rows", "grp"))
+    x = contract_rows(basis_now, basis_now)
+    parts = lax.all_gather(x, ("rows", "grp"), axis=0, tiled=False)
+    gram_basis = parts.sum(axis=0)
     for batch in range(BATCHES):
         columns = lax.all_to_all(snapshots[batch], "grp", split_axis=1, concat_axis=0, tiled=True)
         raw = columns.astype(jnp.float32)

time: 285 us -> 321 us (1.13)
  blocking collectives: 164 us -> 205 us
  waiting for transfers between devices: 4.15 us -> 0.01 us
    all_gather x0 -> x1, blocking collectives: none -> 44.4 us  [body(): parts = lax.all_gather(x, ('rows', 'grp'), axis=0, tiled=False)]
    psum x1 -> x0, blocking collectives: 42.1 us -> none  [body(): gram_basis = lax.psum(contract_rows(basis_now, basis_now), ('rows', 'grp'))]
    psum x3 -> x4, blocking collectives: 122 us -> 161 us  [body(): lax.psum((contract_rows(basis_now, raw), contract_rows(raw, raw)), ('rows...]
    all_to_all x4, waiting for transfers between devices: 4.15 us -> 0.01 us  [body(): lax.all_to_all(snapshots[batch], 'grp', split_axis=1, concat_axis=0, tile...]
  transfers between devices with their start and end apart: 4 -> 4, of which waited for: 1 -> 0; matrix products, arithmetic and copies ran while one was open for 24% -> 21% of each run, Pallas kernels for 0% -> 0%
where the time goes in v1:
time: 321 us; the launch traced here: 320 us
  blocking collectives  205 us (64%)
  other arithmetic  71.8 us (22%)
  matrix products  20.3 us (6%)
  starting transfers between devices  14.8 us (5%)
  local copies, waits for them, and re-layouts  7.12 us (2%)
    psum x4, blocking collectives, body(): lax.psum((contract_rows(basis_now, raw), contract_rows(raw, raw)), ('rows...  161 us
    all_gather x1, blocking collectives, body(): parts = lax.all_gather(x, ('rows', 'grp'), axis=0, tiled=False)  44.4 us
    another operation x16, other arithmetic, lower_solve(): lax.linalg.triangular_solve(factor, right, left_side=True, lower=True)  24.7 us
    all_to_all x4, starting transfers between devices, body(): lax.all_to_all(snapshots[batch], 'grp', split_axis=1, concat_axis=0, tile...  14.8 us
    another operation x12, other arithmetic, small_update(): jnp.linalg.cholesky(matmul(rotation.T, matmul(moment, rotation)))  14.7 us
    another operation x12, other arithmetic, small_update(): factor = jnp.linalg.cholesky(matmul(leading.T, leading))  14.4 us
    another operation x12, other arithmetic, body(): lower = jnp.linalg.cholesky(gram)  14.4 us
    dot_general x54, matrix products, matmul(): jnp.dot(left, right, precision=lax.Precision.HIGHEST, preferred_element_t...  13.7 us
  transfers between devices with their start and end apart: 4, of which 0 were waited for; matrix products, arithmetic and copies ran while one was open for 21% of the time, Pallas kernels for 0%

profile of v1, /device:TPU:0, one launch (start us, length us, event | category | flops | bytes accessed | tf_op | source)
XLA Modules:
  0.0 320.3 jit_solution(8264040308730307779)
XLA Ops:
  0.6 1.9 fusion.229
  2.6 4.4 %all-to-all-start = ((bf16[8,4,2048]{2,0,1:T(8,128)(2,1)}), bf16[8,4,2048]{2,0,1:T(8,128)(2,1)S(1)}, u32[]{:S(2)}, u32[]{:S(2)}) async-start(bf16[8,4,2048]{2,0,1:T(8,128)(2,1)} %bitcast), calls=%async_computation | async-start | bytes 262144 | tf_op jit(solution)/shard_map/all_to_all | solution.py:51
  7.4 44.4 %all-gather = f32[1024,32]{1,0:T(8,128)S(1)} all-gather(f32[32,32]{1,0:T(8,128)S(1)} %fusion.230), channel_id=2, replica_groups=mesh['rows'=8,'grp'=4] {'rows','grp'}, dimensions={0}, use_global_device_ids=true | all-gather | bytes 135168 | tf_op jit(solution)/shard_map/all_gather | solution.py:48
  51.8 3.3 %all-to-all-start.1 = ((bf16[8,4,2048]{2,0,1:T(8,128)(2,1)}), bf16[8,4,2048]{2,0,1:T(8,128)(2,1)S(1)}, u32[]{:S(2)}, u32[]{:S(2)}) async-start(bf16[8,4,2048]{2,0,1:T(8,128)(2,1)} %bitcast.16), calls=%async_computation.1 | async-start | bytes 262144 | tf_op jit(solution)/shard_map/all_to_all | solution.py:51
  55.6 37.2 %all-reduce.7 = (f32[32,32]{0,1:T(8,128)S(1)}, f32[32,32]{0,1:T(8,128)S(1)}) all-reduce(f32[32,32]{0,1:T(8,128)S(1)} %fusion.18, f32[32,32]{0,1:T(8,128)S(1)} %fusion.16), channel_id=1, replica_groups=mesh['rows'=8,'grp'=4] {'rows','grp'}, use_global_device_ids=true, to_apply=%region_0.0 | all-reduce | flops 2048 | bytes 16384 | tf_op jit(solution)/shard_map/psum | solution.py:53
  94.7 2.9 cholesky.194
  99.0 2.4 custom-call.34
  102.6 2.9 cholesky.205
  106.8 2.4 custom-call.33
  111.9 3.5 %all-to-all-start.2 = ((bf16[8,4,2048]{2,0,1:T(8,128)(2,1)}), bf16[8,4,2048]{2,0,1:T(8,128)(2,1)S(1)}, u32[]{:S(2)}, u32[]{:S(2)}) async-start(bf16[8,4,2048]{2,0,1:T(8,128)(2,1)} %bitcast.40), calls=%async_computation.2 | async-start | bytes 262144 | tf_op jit(solution)/shard_map/all_to_all | solution.py:51
  115.8 42.8 %all-reduce.6 = (f32[32,32]{0,1:T(8,128)S(1)}, f32[32,32]{0,1:T(8,128)S(1)}) all-reduce(f32[32,32]{0,1:T(8,128)S(1)} %fusion.14, f32[32,32]{0,1:T(8,128)S(1)} %fusion.12), channel_id=1, replica_groups=mesh['rows'=8,'grp'=4] {'rows','grp'}, use_global_device_ids=true, to_apply=%region_5.9 | all-reduce | flops 2048 | bytes 16384 | tf_op jit(solution)/shard_map/psum | solution.py:53
  160.2 2.9 cholesky.216
  165.3 2.9 cholesky.227
  169.5 2.4 custom-call.39
  173.1 2.9 cholesky.238
  177.4 2.4 custom-call.38
  182.4 3.5 %all-to-all-start.3 = ((bf16[8,4,2048]{2,0,1:T(8,128)(2,1)}), bf16[8,4,2048]{2,0,1:T(8,128)(2,1)S(1)}, u32[]{:S(2)}, u32[]{:S(2)}) async-start(bf16[8,4,2048]{2,0,1:T(8,128)(2,1)} %bitcast.64), calls=%async_computation.3 | async-start | bytes 262144 | tf_op jit(solution)/shard_map/all_to_all | solution.py:51
  186.4 40.1 %all-reduce.5 = (f32[32,32]{0,1:T(8,128)S(1)}, f32[32,32]{0,1:T(8,128)S(1)}) all-reduce(f32[32,32]{0,1:T(8,128)S(1)} %fusion.10, f32[32,32]{0,1:T(8,128)S(1)} %fusion.8), channel_id=1, replica_groups=mesh['rows'=8,'grp'=4] {'rows','grp'}, use_global_device_ids=true, to_apply=%region_7.12 | all-reduce | flops 2048 | bytes 16384 | tf_op jit(solution)/shard_map/psum | solution.py:53
  228.0 2.9 cholesky.249
  233.1 2.9 cholesky.260
  237.3 2.4 custom-call.44
  240.9 2.9 cholesky.271
  245.2 2.4 custom-call.43
  250.7 40.5 %all-reduce.4 = (f32[32,32]{0,1:T(8,128)S(1)}, f32[32,32]{0,1:T(8,128)S(1)}) all-reduce(f32[32,32]{0,1:T(8,128)S(1)} %fusion.6, f32[32,32]{0,1:T(8,128)S(1)} %fusion.4), channel_id=1, replica_groups=mesh['rows'=8,'grp'=4] {'rows','grp'}, use_global_device_ids=true, to_apply=%region_9.14 | all-reduce | flops 2048 | bytes 16384 | tf_op jit(solution)/shard_map/psum | solution.py:53
  292.8 2.9 cholesky.282
  298.5 2.9 cholesky.293
  302.7 2.4 custom-call.49
  305.7 2.9 cholesky.304
  310.0 2.4 custom-call.48
  313.2 2.9 cholesky.315
  316.8 1.3 select_select_fusion.4
  319.2 1.1 convolution_add_fusion
  (172 shorter events, 40.3 us)
Async XLA Ops:
  0.6 6.4 %copy-start = (f32[32,2048]{1,0:T(8,128)S(1)}, f32[32,2048]{1,0:T(8,128)}, u32[]{:S(2)}) copy-start(f32[32,2048]{1,0:T(8,128)} %param.10) | copy-start | bytes 786436
  2.6 4.4 %copy-start.1 = (f32[32,32]{1,0:T(8,128)S(1)}, f32[32,32]{1,0:T(8,128)}, u32[]{:S(2)}) copy-start(f32[32,32]{1,0:T(8,128)} %param.11) | copy-start | bytes 12292
  2.6 49.2 %all-to-all-start = ((bf16[8,4,2048]{2,0,1:T(8,128)(2,1)}), bf16[8,4,2048]{2,0,1:T(8,128)(2,1)S(1)}, u32[]{:S(2)}, u32[]{:S(2)}) async-start(bf16[8,4,2048]{2,0,1:T(8,128)(2,1)} %bitcast), calls=%async_computation | async-start | bytes 262144 | tf_op jit(solution)/shard_map/all_to_all | solution.py:51
  51.8 60.1 %all-to-all-start.1 = ((bf16[8,4,2048]{2,0,1:T(8,128)(2,1)}), bf16[8,4,2048]{2,0,1:T(8,128)(2,1)S(1)}, u32[]{:S(2)}, u32[]{:S(2)}) async-start(bf16[8,4,2048]{2,0,1:T(8,128)(2,1)} %bitcast.16), calls=%async_computation.1 | async-start | bytes 262144 | tf_op jit(solution)/shard_map/all_to_all | solution.py:51
  111.9 70.5 %all-to-all-start.2 = ((bf16[8,4,2048]{2,0,1:T(8,128)(2,1)}), bf16[8,4,2048]{2,0,1:T(8,128)(2,1)S(1)}, u32[]{:S(2)}, u32[]{:S(2)}) async-start(bf16[8,4,2048]{2,0,1:T(8,128)(2,1)} %bitcast.40), calls=%async_computation.2 | async-start | bytes 262144 | tf_op jit(solution)/shard_map/all_to_all | solution.py:51
  182.4 67.8 %all-to-all-start.3 = ((bf16[8,4,2048]{2,0,1:T(8,128)(2,1)}), bf16[8,4,2048]{2,0,1:T(8,128)(2,1)S(1)}, u32[]{:S(2)}, u32[]{:S(2)}) async-start(bf16[8,4,2048]{2,0,1:T(8,128)(2,1)} %bitcast.64), calls=%async_computation.3 | async-start | bytes 262144 | tf_op jit(solution)/shard_map/all_to_all | solution.py:51
